TPU v7x, 32 devices: a whole 2x2x4 slice. The times are simulated.
32 devices in a mesh: data: 2 (over x), inner: 4 (over z), stage: 4 (over y, core).
Axes of the slice: x: 2, y: 2, z: 4, core: 2. Of those that a mesh axis runs over, the one named last changes fastest.
Arguments:
- x: bfloat16 [8, 2048, 1024], P(('data', 'stage'), 'inner'), parts along dimension 0
- g: bfloat16 [8, 2048, 1024], P(('data', 'stage'), 'inner'), parts along dimension 0
- w1: bfloat16 [1, 4, 1024, 4096], P(None, 'stage')
- w2: bfloat16 [1, 4, 4096, 1024], P(None, 'stage')
Outputs:
- output 1: bfloat16 [8, 2048, 1024], P(('data', 'stage'), 'inner'), parts along dimension 0
- output 2: bfloat16 [8, 2048, 1024], P(('data', 'stage'), 'inner'), parts along dimension 0
- output 3: float32 [2, 4, 1024, 4096], P('data', 'stage'), parts along dimension 0
- output 4: float32 [2, 4, 4096, 1024], P('data', 'stage'), parts along dimension 0
There are 2 independent parts. A program takes and returns all parts, laid end to end along the dimension named above; an argument that names none is the same for every part.
All inputs are finite; a program needn't handle non-finite values.
Results may differ from a plain program's by a relative error of at most 0.0126514.
Values are sent between devices in bfloat16 or wider.
A program may use at most 1 GiB of HBM per device.

v0:
```python
import jax
import jax.numpy as jnp
from jax import lax
from jax.sharding import PartitionSpec as P


def _gelu(t):
    return jax.nn.gelu(t, approximate=True)


def _fwd(h, w1, w2):
    z = jnp.dot(h, w1, preferred_element_type=jnp.float32)
    a = _gelu(z).astype(jnp.bfloat16)
    u = jnp.dot(a, w2, preferred_element_type=jnp.float32)
    return (h.astype(jnp.float32) + u).astype(jnp.bfloat16)


def _bwd(h, dh, w1, w2):
    z = jnp.dot(h, w1, preferred_element_type=jnp.float32)
    a32, gelu_vjp = jax.vjp(_gelu, z)
    a = a32.astype(jnp.bfloat16)
    dw2 = jnp.dot(a.T, dh, preferred_element_type=jnp.float32)
    da = jnp.dot(dh, w2.T, preferred_element_type=jnp.float32)
    dz = gelu_vjp(da)[0].astype(jnp.bfloat16)
    dw1 = jnp.dot(h.T, dz, preferred_element_type=jnp.float32)
    dh_prev = (dh.astype(jnp.float32) + jnp.dot(dz, w1.T, preferred_element_type=jnp.float32)).astype(jnp.bfloat16)
    return dh_prev, dw1, dw2


def solution(mesh):
    n_stage = mesh.shape["stage"]
    fwd_perm = [(i, (i + 1) % n_stage) for i in range(n_stage)]
    bwd_perm = [(i, (i - 1) % n_stage) for i in range(n_stage)]

    def body(x, g, w1, w2):
        p = lax.axis_index("stage")
        q = n_stage - 1 - p
        nv, k, d, f = w1.shape
        mb, bl, _ = x.shape
        m = mb * n_stage
        n_ticks = nv * m + n_stage - 1
        x_all = lax.all_gather(x, "stage", axis=0, tiled=True)
        g_all = lax.all_gather(g, "stage", axis=0, tiled=True)

        def slot(s):
            valid = (s >= 0) & (s < nv * m)
            sc = jnp.clip(s, 0, nv * m - 1)
            return valid, sc // m, sc % m

        def fwd_tick(carry, t):
            inc, buf, saved, y_all = carry
            ok_in, _, m_in = slot(t - n_stage)
            buf = buf.at[m_in].set(jnp.where(ok_in & (p == 0), inc, buf[m_in]))
            ok, v, mi = slot(t - p)
            h = jnp.where(p == 0, jnp.where(v == 0, x_all[mi], buf[mi]), inc)
            w1v, w2v = w1[v], w2[v]
            hs = []
            for j in range(k):
                hs.append(h)
                h = _fwd(h, w1v[j], w2v[j])
            saved = saved.at[v, mi].set(jnp.where(ok, jnp.stack(hs), saved[v, mi]))
            last = ok & (p == n_stage - 1) & (v == nv - 1)
            y_all = y_all.at[mi].set(jnp.where(last, h, y_all[mi]))
            inc = lax.ppermute(h, "stage", fwd_perm)
            return (inc, buf, saved, y_all), None

        act0 = jnp.zeros((bl, d), jnp.bfloat16)
        per_mb0 = jnp.zeros((m, bl, d), jnp.bfloat16)
        saved0 = jnp.zeros((nv, m, k, bl, d), jnp.bfloat16)
        ticks = jnp.arange(n_ticks, dtype=jnp.int32)
        (_, _, saved, y_all), _ = lax.scan(fwd_tick, (act0, per_mb0, saved0, per_mb0), ticks)

        def bwd_tick(carry, t):
            inc, buf, dw1, dw2, dx_all = carry
            ok_in, _, m_in = slot(t - n_stage)
            buf = buf.at[m_in].set(jnp.where(ok_in & (q == 0), inc, buf[m_in]))
            ok, u, mi = slot(t - q)
            v = nv - 1 - u
            dh = jnp.where(q == 0, jnp.where(u == 0, g_all[mi], buf[mi]), inc)
            hs = saved[v, mi]
            w1v, w2v = w1[v], w2[v]
            d1s = [None] * k
            d2s = [None] * k
            for j in reversed(range(k)):
                dh, d1s[j], d2s[j] = _bwd(hs[j], dh, w1v[j], w2v[j])
            on = ok.astype(jnp.float32)
            dw1 = dw1.at[v].add(jnp.stack(d1s) * on)
            dw2 = dw2.at[v].add(jnp.stack(d2s) * on)
            first = ok & (p == 0) & (v == 0)
            dx_all = dx_all.at[mi].set(jnp.where(first, dh, dx_all[mi]))
            inc = lax.ppermute(dh, "stage", bwd_perm)
            return (inc, buf, dw1, dw2, dx_all), None

        dw1_0 = jnp.zeros((nv, k, d, f), jnp.float32)
        dw2_0 = jnp.zeros((nv, k, f, d), jnp.float32)
        (_, _, dw1, dw2, dx_all), _ = lax.scan(bwd_tick, (act0, per_mb0, dw1_0, dw2_0, per_mb0), ticks)

        zero = jnp.zeros_like(y_all)
        y = lax.psum_scatter(jnp.where(p == n_stage - 1, y_all, zero), "stage", scatter_dimension=0, tiled=True)
        dx = lax.psum_scatter(jnp.where(p == 0, dx_all, zero), "stage", scatter_dimension=0, tiled=True)
        dw1 = lax.psum(dw1, "inner")
        dw2 = lax.psum(dw2, "inner")
        return y, dx, dw1, dw2

    tok = P(("data", "stage"), "inner", None)
    wsp = P(None, "stage", None, None)
    dsp = P("data", "stage", None, None)
    return jax.shard_map(body, mesh=mesh, in_specs=(tok, tok, wsp, wsp), out_specs=(tok, tok, dsp, dsp), check_vma=False)
```

profile of v0, /device:TPU:0, one launch (start us, length us, event | category | flops | bytes accessed | tf_op | source)
XLA Modules:
  0.0 2046.5 jit_solution(7769755402913369429)
XLA Ops:
  8.8 37.9 %all-gather.3.cloned.1.call-done = bf16[4,512,1024]{2,1,0:T(8,128)(2,1)} async-done(((bf16[1,512,1024]{2,1,0:T(8,128)(2,1)}), bf16[4,512,1024]{2,1,0:T(8,128)(2,1)}) %all-gather.3.cloned.1.call-update) | async-done | bytes 4194320 | tf_op jit(solution)/shard_map/all_gather | solution.py:42
  54.2 316.5 %while.46 = (s32[]{:T(128)}, bf16[512,1024]{1,0:T(8,128)(2,1)S(1)}, bf16[4,512,1024]{2,1,0:T(8,128)(2,1)}, bf16[1,4,1,512,1024]{4,3,2,1,0:T(8,128)(2,1)}, bf16[4...) while((s32[]{:T(128)}, bf16[512,1024]{1,0:T(8,128)(2,1)S(1)}, ...), condition=%wide.region_4.5_spmd, body=%wide.region_0.4_spmd.sunk | while | flops 8614576128 | bytes 41947908 | solution.py:71
  68.1 17.2 fusion.94
  85.5 14.0 collective-permute-done
  113.4 17.1 fusion.94
  130.5 14.2 collective-permute-done
  158.6 17.1 fusion.94
  175.7 14.2 collective-permute-done
  203.8 17.1 fusion.94
  220.9 14.2 collective-permute-done
  249.0 17.1 fusion.94
  266.0 14.2 collective-permute-done
  294.2 17.1 fusion.94
  311.3 14.2 collective-permute-done
  339.4 17.1 fusion.94
  356.5 14.2 collective-permute-done
  378.3 487.9 %while.47 = (s32[]{:T(128)}, bf16[512,1024]{1,0:T(8,128)(2,1)S(1)}, bf16[4,512,1024]{2,1,0:T(8,128)(2,1)}, f32[1,1,1024,4096]{3,2,1,0:T(8,128)}, f32[1,1,4096,10...) while((s32[]{:T(128)}, bf16[512,1024]{1,0:T(8,128)(2,1)S(1)}, ...), condition=%wide.region_10.11_spmd.clone, body=%wide.region_6.10_spmd.clone.sunk | while | flops 21573926912 | bytes 212865904 | solution.py:96
  381.5 11.5 fusion.104
  399.1 12.6 fusion.105
  420.3 13.4 add_select_fusion.5
  433.7 11.0 add_select_fusion.4
  447.9 11.5 fusion.104
  465.4 12.6 fusion.105
  485.2 16.0 add_select_fusion.5
  501.2 13.3 add_select_fusion.4
  517.8 11.5 fusion.104
  535.3 12.6 fusion.105
  555.1 16.0 add_select_fusion.5
  571.1 13.3 add_select_fusion.4
  587.7 11.5 fusion.104
  605.2 12.6 fusion.105
  625.7 16.0 add_select_fusion.5
  641.7 13.3 add_select_fusion.4
  658.2 11.5 fusion.104
  675.8 12.6 fusion.105
  697.0 16.0 add_select_fusion.5
  713.0 13.3 add_select_fusion.4
  729.6 11.5 fusion.104
  747.1 12.6 fusion.105
  766.9 16.0 add_select_fusion.5
  782.9 13.3 add_select_fusion.4
  799.5 11.5 fusion.104
  817.0 12.6 fusion.105
  836.8 16.0 add_select_fusion.5
  852.8 13.3 add_select_fusion.4
  871.2 43.4 %reduce-scatter.5.cloned.1.call-done = bf16[1,512,1024]{2,1,0:T(8,128)(2,1)} async-done(((bf16[4,512,1024]{2,1,0:T(8,128)(2,1)}), bf16[1,512,1024]{2,1,0:T(8,128)(2,1)}) %reduce-scatter.5.cloned.1.call-update) | async-done | bytes 1048592 | tf_op jit(solution)/shard_map/reduce_scatter | solution.py:100
  914.6 1102.8 %all-reduce.3.cloned.1.call-done = (f32[1,1,1024,4096]{3,2,1,0:T(8,128)}, f32[1,1,4096,1024]{3,2,1,0:T(8,128)}) async-done(((f32[1,1,1024,4096]{3,2,1,0:T(8,128)}, f32[1,1,4096,1024]{3,2,1,0:T(8,128)}), (f32[1,1,1024,4096]{3,2,1,0:T(8,128)}, f32[1,1,4096,1024]{3,2,1,0:T(8,128)})) %all-reduce.3.cloned.1.call-update) | async-done | bytes 33554448 | tf_op jit(solution)/shard_map/psum | solution.py:101
  2017.4 12.6 copy.48
  (221 shorter events, 229.1 us)
Async XLA Ops:
  7.2 47.1 %copy-start.1 = (s32[3]{0:T(128)S(1)}, s32[3]{0:T(128)}, u32[]{:S(2)}) copy-start(s32[3]{0:T(128)} %constant.338.clone.1) | copy-start | bytes 40
  7.2 47.0 %copy-start.2 = (s32[5]{0:T(128)S(1)}, s32[5]{0:T(128)}, u32[]{:S(2)}) copy-start(s32[5]{0:T(128)} %constant.344.clone.1) | copy-start | bytes 64
  7.2 39.4 %all-gather.3.cloned.1.call-start = ((), (), s32[]{:S(2)}) async-start(), calls=%async_computation.2 | async-start | bytes 5242880 | tf_op jit(solution)/shard_map/all_gather | solution.py:42
  7.9 365.2 %all-gather.5.cloned.1.call-start = ((), (), s32[]{:S(2)}) async-start(), calls=%async_computation.4 | async-start | bytes 5242880 | tf_op jit(solution)/shard_map/all_gather | solution.py:43
  8.7 862.5 %reduce-scatter.3.cloned.1.call-start = ((), (), s32[]{:S(2)}) async-start(), calls=%async_computation.3 | async-start | bytes 5242880 | tf_op jit(solution)/shard_map/reduce_scatter | solution.py:99
  85.3 14.2 collective-permute-start
  130.5 14.2 collective-permute-start
  175.7 14.2 collective-permute-start
  220.9 14.2 collective-permute-start
  266.0 14.2 collective-permute-start
  311.3 14.2 collective-permute-start
  356.5 14.2 collective-permute-start
  373.1 541.5 %reduce-scatter.5.cloned.1.call-start = ((), (), s32[]{:S(2)}) async-start(), calls=%async_computation.5 | async-start | bytes 5242880 | tf_op jit(solution)/shard_map/reduce_scatter | solution.py:100
  397.2 14.4 slice-start
  399.1 12.6 slice-start.1
  411.7 6.5 copy-start.3
  418.1 26.5 %collective-permute-start.1 = (bf16[512,1024]{1,0:T(8,128)(2,1)S(1)}, bf16[512,1024]{1,0:T(8,128)(2,1)S(1)}, u32[]{:S(2)}, u32[]{:S(2)}) collective-permute-start(bf16[512,1024]{1,0:T(8,128)(2,1)S(1)} %get-tuple-element.707), channel_id=1, source_target_pairs={{0,3},{1,0},{2,1},{3,2},{4,7},{5,4},{6,5},{7,6},{8,11},{9,8},{10,9... | collective-permute-start | bytes 3145736 | tf_op jit(solution)/shard_map/while/body/eval_jaxpr/ppermute | solution.py:91
  420.3 13.4 copy-start.4
  463.6 14.4 slice-start
  465.4 12.6 slice-start.1
  478.0 6.5 copy-start.3
  484.5 30.1 %collective-permute-start.1 = (bf16[512,1024]{1,0:T(8,128)(2,1)S(1)}, bf16[512,1024]{1,0:T(8,128)(2,1)S(1)}, u32[]{:S(2)}, u32[]{:S(2)}) collective-permute-start(bf16[512,1024]{1,0:T(8,128)(2,1)S(1)} %get-tuple-element.707), channel_id=1, source_target_pairs={{0,3},{1,0},{2,1},{3,2},{4,7},{5,4},{6,5},{7,6},{8,11},{9,8},{10,9... | collective-permute-start | bytes 3145736 | tf_op jit(solution)/shard_map/while/body/eval_jaxpr/ppermute | solution.py:91
  485.2 16.0 copy-start.4
  533.5 14.4 slice-start
  535.3 12.6 slice-start.1
  547.9 6.5 copy-start.3
  554.4 30.1 %collective-permute-start.1 = (bf16[512,1024]{1,0:T(8,128)(2,1)S(1)}, bf16[512,1024]{1,0:T(8,128)(2,1)S(1)}, u32[]{:S(2)}, u32[]{:S(2)}) collective-permute-start(bf16[512,1024]{1,0:T(8,128)(2,1)S(1)} %get-tuple-element.707), channel_id=1, source_target_pairs={{0,3},{1,0},{2,1},{3,2},{4,7},{5,4},{6,5},{7,6},{8,11},{9,8},{10,9... | collective-permute-start | bytes 3145736 | tf_op jit(solution)/shard_map/while/body/eval_jaxpr/ppermute | solution.py:91
  555.1 16.0 copy-start.4
  603.4 14.4 slice-start
  605.2 12.6 slice-start.1
  617.8 6.5 copy-start.3
  624.3 30.7 %collective-permute-start.1 = (bf16[512,1024]{1,0:T(8,128)(2,1)S(1)}, bf16[512,1024]{1,0:T(8,128)(2,1)S(1)}, u32[]{:S(2)}, u32[]{:S(2)}) collective-permute-start(bf16[512,1024]{1,0:T(8,128)(2,1)S(1)} %get-tuple-element.707), channel_id=1, source_target_pairs={{0,3},{1,0},{2,1},{3,2},{4,7},{5,4},{6,5},{7,6},{8,11},{9,8},{10,9... | collective-permute-start | bytes 3145736 | tf_op jit(solution)/shard_map/while/body/eval_jaxpr/ppermute | solution.py:91
  625.7 16.0 copy-start.4
  673.9 14.4 slice-start
  675.8 12.6 slice-start.1
  694.7 31.6 %collective-permute-start.1 = (bf16[512,1024]{1,0:T(8,128)(2,1)S(1)}, bf16[512,1024]{1,0:T(8,128)(2,1)S(1)}, u32[]{:S(2)}, u32[]{:S(2)}) collective-permute-start(bf16[512,1024]{1,0:T(8,128)(2,1)S(1)} %get-tuple-element.707), channel_id=1, source_target_pairs={{0,3},{1,0},{2,1},{3,2},{4,7},{5,4},{6,5},{7,6},{8,11},{9,8},{10,9... | collective-permute-start | bytes 3145736 | tf_op jit(solution)/shard_map/while/body/eval_jaxpr/ppermute | solution.py:91
  697.0 16.0 copy-start.4
  745.3 14.4 slice-start
  747.1 12.6 slice-start.1
  766.1 30.1 %collective-permute-start.1 = (bf16[512,1024]{1,0:T(8,128)(2,1)S(1)}, bf16[512,1024]{1,0:T(8,128)(2,1)S(1)}, u32[]{:S(2)}, u32[]{:S(2)}) collective-permute-start(bf16[512,1024]{1,0:T(8,128)(2,1)S(1)} %get-tuple-element.707), channel_id=1, source_target_pairs={{0,3},{1,0},{2,1},{3,2},{4,7},{5,4},{6,5},{7,6},{8,11},{9,8},{10,9... | collective-permute-start | bytes 3145736 | tf_op jit(solution)/shard_map/while/body/eval_jaxpr/ppermute | solution.py:91
  766.9 16.0 copy-start.4
  815.2 14.4 slice-start
  817.0 12.6 slice-start.1
  829.6 6.4 copy-start.3
  836.0 30.1 %collective-permute-start.1 = (bf16[512,1024]{1,0:T(8,128)(2,1)S(1)}, bf16[512,1024]{1,0:T(8,128)(2,1)S(1)}, u32[]{:S(2)}, u32[]{:S(2)}) collective-permute-start(bf16[512,1024]{1,0:T(8,128)(2,1)S(1)} %get-tuple-element.707), channel_id=1, source_target_pairs={{0,3},{1,0},{2,1},{3,2},{4,7},{5,4},{6,5},{7,6},{8,11},{9,8},{10,9... | collective-permute-start | bytes 3145736 | tf_op jit(solution)/shard_map/while/body/eval_jaxpr/ppermute | solution.py:91
  836.8 16.0 copy-start.4
  870.6 1146.8 %all-reduce.3.cloned.1.call-start = ((), (), s32[]{:S(2)}) async-start(), calls=%async_computation.6 | async-start | bytes 67108864 | tf_op jit(solution)/shard_map/psum | solution.py:101
  2017.4 16.4 copy-start
  (2 other events, 12.8 us)
Sparse Core Ops, SparseCore 0:
  9.6 37.0 all-gather.2
  48.2 34.2 all-gather.4
  373.2 44.7 reduce-scatter.2
  870.7 43.8 reduce-scatter.4
  917.7 1099.6 all-reduce.2
where the time goes:
time: 2050 us
  waiting for transfers between devices  1290 us (63%)
  matrix products  533 us (26%)
  other arithmetic  119 us (6%)
  local copies, waits for them, and re-layouts  71.4 us (3%)
    psum x1, waiting for transfers between devices, body(): dw1 = lax.psum(dw1, 'inner')  1100 us
    dot_general x7, matrix products, _fwd(): u = jnp.dot(a, w2, preferred_element_type=jnp.float32)  120 us
    dot_general x7, matrix products, _bwd(): dw2 = jnp.dot(a.T, dh, preferred_element_type=jnp.float32)  109 us
    ppermute x7, waiting for transfers between devices, fwd_tick(): inc = lax.ppermute(h, 'stage', fwd_perm)  99.3 us
    dot_general x7, matrix products, _bwd(): dw1 = jnp.dot(h.T, dz, preferred_element_type=jnp.float32)  91 us
    dot_general x7, matrix products, _bwd(): da = jnp.dot(dh, w2.T, preferred_element_type=jnp.float32)  88 us
    dot_general x7, matrix products, _bwd(): z = jnp.dot(h, w1, preferred_element_type=jnp.float32)  80.2 us
    dot_general x7, matrix products, _bwd(): jnp.dot(dz, w1.T, preferred_element_type=jnp.float32)  44.9 us
  transfers between devices with their start and end apart: 19, of which 10 were waited for; matrix products, arithmetic and copies ran while one was open for 34% of the time, Pallas kernels for 0%

commit v1 on v0

v1 whole, which is shorter than its diff:
```python
import functools

import jax
import jax.numpy as jnp
from jax import lax
from jax.experimental import pallas as pl
from jax.experimental.pallas import tpu as pltpu
from jax.sharding import PartitionSpec as P

MESH = pl.DeviceIdType.MESH
F32 = jnp.float32
BF16 = jnp.bfloat16

C = 256
FT = 512
DT = 256
LAG = (11, 8, 4, 1)
X_AT = (0, 0, 4, 4)
G_AT = (0, 8, 8, 16)

C1 = 0.7978845608028654
C2 = 0.044715 * C1


def _gelu_and_slope(z):
    zz = z * z
    s = 0.5 * jnp.tanh(z * (C1 + C2 * zz)) + 0.5
    a = z * s
    slope = s + a * (1.0 - s) * (2.0 * C1 + 6.0 * C2 * zz)
    return a, slope


def _by_stage(p, values):
    out = jnp.int32(values[0])
    for i, v in enumerate(values[1:], 1):
        out = jnp.where(p == i, jnp.int32(v), out)
    return out


def chain_kernel(cfg, x_hbm, g_hbm, w1_hbm, w2_hbm, h_all, g_all, a_all, dz_all, d_all, y_ref, dx_ref,
                 x_ref, g_ref, w1, w2, h_in, g_in, a_st, d_st, d_in, dz_st, h_out, g_out,
                 w_sem, h_sem, g_sem, hl_sem, gl_sem, dl_sem, a_sem, d_sem, dz_sem, hs_sem, gs_sem,
                 xs_sem, gx_sem, y_sem, dx_sem):
    n_stage, n_inner, n, d, f = cfg
    p = lax.axis_index("stage")
    zi = lax.axis_index("inner")
    last = n_stage - 1
    per = n // n_stage
    piece = C // n_inner
    lag = _by_stage(p, LAG)
    x_at = _by_stage(p, X_AT)
    g_at = _by_stage(p, G_AT)

    cx = pltpu.make_async_copy(x_hbm, x_ref, xs_sem)
    cg = pltpu.make_async_copy(g_hbm, g_ref, gx_sem)
    cx.start()
    cg.start()
    cw1 = pltpu.make_async_copy(w1_hbm, w1, w_sem.at[0])
    cw2 = pltpu.make_async_copy(w2_hbm, w2, w_sem.at[1])
    cw1.start()
    cw2.start()

    def hand_out(src, dst, s, sems, send_sem, stage):
        k = p * per + s
        mine = src.at[pl.ds(s * piece, piece), :]
        there = dst.at[k, pl.ds(zi * piece, piece), :]
        for j in range(n_inner):
            here = (p == stage) & (zi == j)

            @pl.when(jnp.logical_not(here))
            def _():
                pltpu.make_async_remote_copy(
                    src_ref=mine, dst_ref=there, send_sem=send_sem, recv_sem=sems.at[k],
                    device_id={"stage": jnp.int32(stage), "inner": jnp.int32(j)}, device_id_type=MESH).start()

            @pl.when(here)
            def _():
                pltpu.make_async_copy(mine, there, sems.at[k]).start()

    def whole(src_slot, dst, k, send_sem, sems, stage):
        return pltpu.make_async_remote_copy(
            src_ref=src_slot, dst_ref=dst.at[k], send_sem=send_sem, recv_sem=sems.at[k],
            device_id={"stage": stage, "inner": zi}, device_id_type=MESH)

    def part(src_slot, dst, k, send_sem, recv_sem, stage, go):
        m, s = lax.div(k, per), lax.rem(k, per)
        mine = src_slot.at[pl.ds(zi * piece, piece), :]
        there = dst.at[pl.ds(s * piece, piece), :]
        if not go:
            pltpu.make_async_copy(mine, there, send_sem).wait()
            return

        @pl.when(m != stage)
        def _():
            pltpu.make_async_remote_copy(
                src_ref=mine, dst_ref=there, send_sem=send_sem, recv_sem=recv_sem,
                device_id={"stage": m, "inner": zi}, device_id_type=MESH).start()

        @pl.when(m == stage)
        def _():
            pltpu.make_async_copy(mine, there, send_sem).start()

    def arrived(buf, sems, k):
        pltpu.make_async_copy(buf.at[k], buf.at[k], sems.at[k]).wait()

    def load_h(k):
        return pltpu.make_async_copy(h_all.at[k], h_in.at[lax.rem(k, 2)], hl_sem.at[lax.rem(k, 2)])

    def load_g(k):
        return pltpu.make_async_copy(g_all.at[k], g_in.at[lax.rem(k, 2)], gl_sem.at[lax.rem(k, 2)])

    def load_d(k):
        return pltpu.make_async_copy(d_all.at[k], d_in, dl_sem)

    def forward(t):
        slot = lax.rem(t, 2)

        load_h(t).wait()
        for j in range(f // FT):
            cols = pl.ds(j * FT, FT)
            z = jnp.dot(h_in[slot], w1[:, cols], preferred_element_type=F32)
            a, slope = _gelu_and_slope(z)
            a_st[:, cols] = a.astype(BF16)
            d_st[:, cols] = slope
        pltpu.make_async_copy(a_st, a_all.at[t], a_sem).start()
        pltpu.make_async_copy(d_st, d_all.at[t], d_sem).start()

        @pl.when(t > 1)
        def _():
            @pl.when(p < last)
            def _():
                whole(h_out.at[slot], h_all, t - 2, hs_sem.at[slot], h_sem, p + 1).wait_send()

            @pl.when(p == last)
            def _():
                part(h_out.at[slot], y_ref, t - 2, hs_sem.at[slot], y_sem, last, False)

        for j in range(d // DT):
            cols = pl.ds(j * DT, DT)
            u = jnp.dot(a_st[...], w2[:, cols], preferred_element_type=F32)
            h_out[slot, :, cols] = (h_in[slot, :, cols].astype(F32) + u).astype(BF16)

        @pl.when(p < last)
        def _():
            whole(h_out.at[slot], h_all, t, hs_sem.at[slot], h_sem, p + 1).start()

        @pl.when(p == last)
        def _():
            part(h_out.at[slot], y_ref, t, hs_sem.at[slot], y_sem, last, True)

    def backward(k):
        slot = lax.rem(k, 2)

        @pl.when(k > 0)
        def _():
            pltpu.make_async_copy(dz_st, dz_all.at[k - 1], dz_sem).wait()

        load_g(k).wait()
        load_d(k).wait()
        nt = (((1,), (1,)), ((), ()))
        for j in range(f // FT):
            cols = pl.ds(j * FT, FT)
            da = lax.dot_general(g_in[slot], w2[cols, :], nt, preferred_element_type=F32)
            dz_st[:, cols] = (da * d_in[:, cols]).astype(BF16)
        pltpu.make_async_copy(dz_st, dz_all.at[k], dz_sem).start()

        @pl.when(k > 1)
        def _():
            @pl.when(p > 0)
            def _():
                whole(g_out.at[slot], g_all, k - 2, gs_sem.at[slot], g_sem, p - 1).wait_send()

            @pl.when(p == 0)
            def _():
                part(g_out.at[slot], dx_ref, k - 2, gs_sem.at[slot], dx_sem, 0, False)

        for j in range(d // DT):
            cols = pl.ds(j * DT, DT)
            dh = lax.dot_general(dz_st[...], w1[cols, :], nt, preferred_element_type=F32)
            g_out[slot, :, cols] = (g_in[slot, :, cols].astype(F32) + dh).astype(BF16)

        @pl.when(p > 0)
        def _():
            whole(g_out.at[slot], g_all, k, gs_sem.at[slot], g_sem, p - 1).start()

        @pl.when(p == 0)
        def _():
            part(g_out.at[slot], dx_ref, k, gs_sem.at[slot], dx_sem, 0, True)

    cx.wait()
    cg.wait()

    @pl.when(p == 0)
    def _():
        for s in range(per):
            hand_out(x_ref, h_all, s, h_sem, xs_sem, 0)

    def step(t, _):
        kb = t - lag
        do_f = t < n
        do_b = (kb >= 0) & (kb < n)
        sx = t - x_at
        sg = t - g_at

        @pl.when((t > 0) & (t <= n))
        def _():
            pltpu.make_async_copy(a_st, a_all.at[t - 1], a_sem).wait()
            pltpu.make_async_copy(d_st, d_all.at[t - 1], d_sem).wait()

        @pl.when((p > 0) & (sx >= 0) & (sx < per))
        def _():
            hand_out(x_ref, h_all, sx, h_sem, xs_sem, 0)

        @pl.when((sg >= 0) & (sg < per))
        def _():
            hand_out(g_ref, g_all, sg, g_sem, gx_sem, last)

        @pl.when(t == 0)
        def _():
            arrived(h_all, h_sem, t)
            load_h(t).start()
            cw1.wait()
            cw2.wait()

        @pl.when(do_b)
        def _():
            arrived(g_all, g_sem, kb)
            load_g(kb).start()

        @pl.when(do_b & (t < n))
        def _():
            load_d(kb).start()

        @pl.when(do_f)
        def _():
            forward(t)

        @pl.when(do_b & (t >= n))
        def _():
            load_d(kb).start()

        @pl.when(t + 1 < n)
        def _():
            arrived(h_all, h_sem, t + 1)
            load_h(t + 1).start()

        @pl.when(do_b)
        def _():
            backward(kb)

        return 0

    lax.fori_loop(0, n + max(LAG), step, 0)

    pltpu.make_async_copy(dz_st, dz_all.at[n - 1], dz_sem).wait()
    for k in (n - 2, n - 1):
        slot = k % 2

        @pl.when(p < last)
        def _():
            whole(h_out.at[slot], h_all, k, hs_sem.at[slot], h_sem, p + 1).wait_send()

        @pl.when(p == last)
        def _():
            part(h_out.at[slot], y_ref, jnp.int32(k), hs_sem.at[slot], y_sem, last, False)

        @pl.when(p > 0)
        def _():
            whole(g_out.at[slot], g_all, k, gs_sem.at[slot], g_sem, p - 1).wait_send()

        @pl.when(p == 0)
        def _():
            part(g_out.at[slot], dx_ref, jnp.int32(k), gs_sem.at[slot], dx_sem, 0, False)

    full = n // n_stage
    less = full * (n_inner - 1) // n_inner
    for buf, sem, stage, out, out_sem, out_stage in (
        (h_all, xs_sem, 0, y_ref, y_sem, last), (g_all, gx_sem, last, dx_ref, dx_sem, 0)):
        @pl.when(p != stage)
        def _():
            pltpu.make_async_copy(buf.at[pl.ds(0, full)], buf.at[pl.ds(0, full)], sem).wait()

        @pl.when(p == stage)
        def _():
            pltpu.make_async_copy(buf.at[pl.ds(0, less)], buf.at[pl.ds(0, less)], sem).wait()

        @pl.when(p != out_stage)
        def _():
            pltpu.make_async_copy(out, out, out_sem).wait()


def chain(cfg, x, g, w1, w2):
    n_stage, n_inner, n, d, f = cfg
    any_ = pl.BlockSpec(memory_space=pl.ANY)
    rows = x.shape[0]
    shape = jax.ShapeDtypeStruct
    dma = pltpu.SemaphoreType.DMA
    return pl.pallas_call(
        functools.partial(chain_kernel, cfg),
        name="chain",
        out_shape=(
            shape((n, C, d), BF16), shape((n, C, d), BF16), shape((n, C, f), BF16), shape((n, C, f), BF16),
            shape((n, C, f), F32), shape((rows, d), BF16), shape((rows, d), BF16),
        ),
        in_specs=[any_] * 4,
        out_specs=(any_,) * 7,
        scratch_shapes=[
            pltpu.VMEM((rows, d), BF16), pltpu.VMEM((rows, d), BF16), pltpu.VMEM((d, f), BF16), pltpu.VMEM((f, d), BF16),
            pltpu.VMEM((2, C, d), BF16), pltpu.VMEM((2, C, d), BF16),
            pltpu.VMEM((C, f), BF16), pltpu.VMEM((C, f), F32), pltpu.VMEM((C, f), F32), pltpu.VMEM((C, f), BF16),
            pltpu.VMEM((2, C, d), BF16), pltpu.VMEM((2, C, d), BF16),
            dma((2,)), dma((n,)), dma((n,)), dma((2,)), dma((2,)), dma, dma, dma, dma, dma((2,)), dma((2,)),
            dma, dma, dma, dma,
        ],
        compiler_params=pltpu.CompilerParams(has_side_effects=True, vmem_limit_bytes=60 * 2**20),
        cost_estimate=pl.CostEstimate(
            flops=8 * n * C * d * f, bytes_accessed=n * C * (f * 14 + d * 8), transcendentals=n * C * f),
    )(x, g, w1, w2)


def solution(mesh):
    n_stage, n_inner = mesh.shape["stage"], mesh.shape["inner"]

    def body(x, g, w1, w2):
        _, rows, d = x.shape
        f = w1.shape[-1]
        n = rows * n_inner * n_stage // C
        cfg = (n_stage, n_inner, n, d, f)
        h_all, g_all, a_all, dz_all, _, y, dx = chain(
            cfg, x.reshape(rows, d), g.reshape(rows, d), w1.reshape(d, f), w2.reshape(f, d))
        tn = (((0,), (0,)), ((), ()))
        h2, g2 = h_all.reshape(n * C, d), g_all.reshape(n * C, d)
        dw1 = lax.dot_general(h2, dz_all.reshape(n * C, f), tn, preferred_element_type=F32)
        dw2 = lax.dot_general(a_all.reshape(n * C, f), g2, tn, preferred_element_type=F32)
        return y.reshape(x.shape), dx.reshape(g.shape), dw1.reshape(1, 1, d, f), dw2.reshape(1, 1, f, d)

    tok = P(("data", "stage"), "inner", None)
    wsp = P(None, "stage", None, None)
    dsp = P("data", "stage", None, None)
    return jax.shard_map(body, mesh=mesh, in_specs=(tok, tok, wsp, wsp), out_specs=(tok, tok, dsp, dsp), check_vma=False)
```

time: 2050 us -> 725 us (0.35)
  waiting for transfers between devices: 1290 us -> 0 us
  Pallas kernels: 0 us -> 560 us
  matrix products: 533 us -> 161 us
  other arithmetic: 119 us -> 0 us
  local copies, waits for them, and re-layouts: 71.4 us -> 1.95 us
    psum x1 -> x0, waiting for transfers between devices: 1100 us -> none  [body(): dw1 = lax.psum(dw1, 'inner')]
    pallas_call x0 -> x1, Pallas kernels: none -> 560 us  [chain(): pl.pallas_call(functools.partial(chain_kernel, cfg), name='chain', out_sh...]
    dot_general x42 -> x2, matrix products: 533 us -> 161 us  [the longest x1 80.4 us: body(): lax.dot_general(h2, dz_all.reshape(n * C, f), tn, preferred_element_type=...]
    ppermute x14 -> x0, waiting for transfers between devices: 99.3 us -> none  [the longest x7 99.3 us: fwd_tick(): inc = lax.ppermute(h, 'stage', fwd_perm)]
    scatter x21 -> x0, other arithmetic: 79.4 us -> none  [the longest x7 31 us: fwd_tick(): saved = saved.at[v, mi].set(jnp.where(ok, jnp.stack(hs), saved[v, mi]))]
    reduce_scatter x2 -> x0, waiting for transfers between devices: 43.4 us -> none  [the longest x1 43.4 us: body(): lax.psum_scatter(jnp.where(p == 0, dx_all, zero), 'stage', scatter_dimens...]
    all_gather x2 -> x0, waiting for transfers between devices: 37.9 us -> none  [the longest x1 37.9 us: body(): x_all = lax.all_gather(x, 'stage', axis=0, tiled=True)]
    dynamic_slice x35 -> x0, local copies, waits for them, and re-layouts: 35.4 us -> none  [the longest x7 9.1 us: fwd_tick(): saved = saved.at[v, mi].set(jnp.where(ok, jnp.stack(hs), saved[v, mi]))]
  transfers between devices with their start and end apart: 19 -> 0, of which waited for: 10 -> 0; matrix products, arithmetic and copies ran while one was open for 34% -> 0% of each run, Pallas kernels for 0% -> 0%
where the time goes in v1:
time: 725 us; the launch traced here: 724 us
  Pallas kernels  560 us (77%)
  matrix products  161 us (22%)
    pallas_call x1, Pallas kernels, chain(): pl.pallas_call(functools.partial(chain_kernel, cfg), name='chain', out_sh...  560 us
    dot_general x1, matrix products, body(): lax.dot_general(h2, dz_all.reshape(n * C, f), tn, preferred_element_type=...  80.4 us
    dot_general x1, matrix products, body(): lax.dot_general(a_all.reshape(n * C, f), g2, tn, preferred_element_type=F32)  80.4 us

profile of v1, /device:TPU:0, one launch (start us, length us, event | category | flops | bytes accessed | tf_op | source)
XLA Modules:
  0.0 723.8 jit_solution(16677256284591481654)
XLA Ops:
  0.6 560.4 %chain.1 = (bf16[32,256,1024]{2,1,0:T(8,128)(2,1)}, bf16[32,256,1024]{2,1,0:T(8,128)(2,1)}, bf16[32,256,4096]{2,1,0:T(8,128)(2,1)}, bf16[32,256,4096]{2,1,0:T(8,...) custom-call(bf16[512,1024]{1,0:T(8,128)(2,1)} %bitcast.22, ...), custom_call_target="tpu_custom_call" | custom-call | flops 274877906944 | bytes 536870912 | tf_op jit(solution)/shard_map/chain/pallas_call | solution.py:298
  561.0 80.4 %convolution_bitcast_fusion.1 = f32[1,1,1024,4096]{3,2,1,0:T(8,128)} fusion(bf16[32,256,1024]{2,1,0:T(8,128)(2,1)} %get-tuple-element.12, bf16[32,256,4096]{2,1,0:T(8,128)(2,1)} %get-tuple-element.13), kind=kOutput, calls=%fused_computation.1 | convolution fusion | flops 68719476736 | bytes 100663296 | tf_op jit(solution)/shard_map/dot_general | solution.py:333
  641.4 0.0 copy-start.1
  641.4 0.0 copy-start
  641.4 80.4 %convolution_bitcast_fusion = f32[1,1,4096,1024]{3,2,1,0:T(8,128)} fusion(bf16[32,256,4096]{2,1,0:T(8,128)(2,1)} %get-tuple-element.14, bf16[32,256,1024]{2,1,0:T(8,128)(2,1)} %get-tuple-element.15), kind=kOutput, calls=%fused_computation | convolution fusion | flops 68719476736 | bytes 100663296 | tf_op jit(solution)/shard_map/dot_general | solution.py:334
  721.9 0.0 copy-done.1
  721.9 1.0 copy.14
  722.8 0.0 copy-done
  722.8 1.0 copy.15
Async XLA Ops:
  641.4 80.4 %copy-start.1 = (bf16[512,1024]{1,0:T(8,128)(2,1)S(1)}, bf16[512,1024]{1,0:T(8,128)(2,1)}, u32[]{:S(2)}) copy-start(bf16[512,1024]{1,0:T(8,128)(2,1)} %get-tuple-element.10) | copy-start | bytes 3145732
  641.4 81.4 %copy-start = (bf16[512,1024]{1,0:T(8,128)(2,1)S(1)}, bf16[512,1024]{1,0:T(8,128)(2,1)}, u32[]{:S(2)}) copy-start(bf16[512,1024]{1,0:T(8,128)(2,1)} %get-tuple-element.11) | copy-start | bytes 3145732
